TPU v7x, 128 devices: a whole 4x4x4 slice. The times are simulated.
128 devices in a mesh: dp: 16 (over x, z_lo, core), tensor: 8 (over y, z_hi).
Axes of the slice: x: 4, y: 4, z: 4 (z_hi: 2, z_lo: 2; z = z_hi * 2 + z_lo), core: 2. Of those that a mesh axis runs over, the one named last changes fastest.
Arguments:
- acts: bfloat16 [16384, 3584], P('dp'), may hold values from -6 to 6
- cotangent: bfloat16 [16384, 18944], P('dp', 'tensor'), may hold values from -6 to 6
- hessian_ema: float32 [3584, 18944], P('dp', 'tensor'), may hold values from 0.02 to 2
- momentum: float32 [3584, 18944], P('dp', 'tensor'), may hold values from -0.12 to 0.12
- gamma_table: float32 [28], replicated, may hold values from 0.005 to 0.02
- layer_index: int32 [1], replicated, may hold values from 0 to 27
- step_count: int32 [1], replicated, may hold values from 1 to 20
Outputs:
- new_hessian: float32 [67895296], P(('dp', 'tensor'))
- ratio: float32 [67895296], P(('dp', 'tensor'))
All inputs are finite; a program needn't handle non-finite values.
Results may differ from a plain program's by a relative error of at most 0.0003.
Values sent between devices are 32-bit elements; how exact they have to be, the bound alone decides.
A program may use at most 128 MiB of HBM per device.

v0:
```python
import jax.numpy as jnp
from jax import lax

LAYERS_ALL = 28
TOKENS = 16384


def reference(acts, cotangent, hessian_ema, momentum, gamma_table, layer_index, step_count):
    grad_sum = lax.dot_general(
        acts, cotangent, (((0,), (0,)), ((), ())), preferred_element_type=jnp.float32
    )
    estimate = grad_sum * grad_sum / float(TOKENS)
    fresh = 0.99 * hessian_ema + 0.01 * estimate
    picks = jnp.arange(LAYERS_ALL, dtype=jnp.int32) == layer_index[0]
    gamma = jnp.sum(jnp.where(picks, gamma_table, jnp.zeros_like(gamma_table)))
    correction = 1.0 - jnp.power(
        jnp.asarray(0.99, gamma_table.dtype), step_count[0].astype(gamma_table.dtype)
    )
    corrected = fresh / correction
    ratio = jnp.clip(momentum / (gamma * corrected), -1.0, 1.0)
    return (fresh.reshape(-1), ratio.reshape(-1))


def solution(mesh):
    return reference
```

profile of v0, /device:TPU:1, one launch (start us, length us, event | category | flops | bytes accessed | tf_op | source)
XLA Modules:
  0.0 489.5 jit_solution(10108396787972284967)
XLA Ops:
  7.2 0.0 reduce-scatter.4.cloned.1.call-start
  7.2 26.2 %fusion.1 = f32[3584,2368]{1,0:T(8,128)} fusion(bf16[1024,3584]{1,0:T(8,128)(2,1)} %param.1, bf16[1024,2368]{0,1:T(8,128)(2,1)} %param.2), kind=kOutput, calls=%fused_computation.4 | convolution fusion | flops 17381195776 | bytes 46137344 | tf_op jit(solution)/dot_general | solution.py:9
  33.4 0.0 copy-start
  33.4 0.0 reduce-scatter.4.cloned.1.call-update
  34.7 0.0 copy-done
  34.7 0.7 fusion
  35.4 363.9 %reduce-scatter.4.cloned.1.call-done = f32[224,2368]{1,0:T(8,128)} async-done(((f32[3584,2368]{1,0:T(8,128)}), f32[224,2368]{1,0:T(8,128)}) %reduce-scatter.4.cloned.1.call-update) | async-done | bytes 2121744
  399.3 5.5 %divide_clamp_fusion = (f32[224,2368]{1,0:T(8,128)}, f32[224,2368]{1,0:T(8,128)S(1)}) fusion(f32[224,2368]{1,0:T(8,128)} %param.3, f32[]{:T(128)} %bitcast.3, f32[]{:T(128)} %fusion, f32[224,2368]{1,0:T(8,128)} %reduce-scatter.4.cloned.1.call-done, f32[224,2368]{1,0:T(8,128)} %param), kind=kLoop, calls=%fused_computation | loop fusion | flops 4243456 | bytes 10608648 | tf_op jit(solution)/jit(clip)/min | solution.py:20
  404.9 3.1 reshape.51
  408.0 6.3 %all-to-all-start = ((f32[1,8,28,2368]{3,0,2,1:T(1,128)}), f32[1,8,28,2368]{3,0,2,1:T(1,128)S(1)}, u32[]{:S(2)}, u32[]{:S(2)}) async-start(f32[1,8,28,2368]{3,0,2,1:T(1,128)} %reshape.51), calls=%async_computation | async-start | bytes 4358144 | tf_op jit(solution)/add | solution.py:13
  414.3 4.4 reshape.52
  418.7 23.7 %all-to-all-done = f32[1,8,28,2368]{3,0,2,1:T(1,128)S(1)} async-done(((f32[1,8,28,2368]{3,0,2,1:T(1,128)}), f32[1,8,28,2368]{3,0,2,1:T(1,128)S(1)}, u32[]{:S(2)}, u32[]{:S(2)}) %all-to-all-start) | async-done | bytes 2121760 | tf_op jit(solution)/add | solution.py:13
  442.4 4.4 all-to-all-start.1
  446.8 1.5 copy.3
  448.3 3.4 reshape.27
  451.7 26.7 %all-to-all-done.1 = f32[1,8,28,2368]{3,0,2,1:T(1,128)} async-done(((f32[1,8,28,2368]{3,0,2,1:T(1,128)}), f32[1,8,28,2368]{3,0,2,1:T(1,128)}, u32[]{:S(2)}, u32[]{:S(2)}) %all-to-all-start.1) | async-done | bytes 2121760 | tf_op jit(solution)/jit(clip)/min | solution.py:20
  478.5 1.8 copy.5
  480.2 2.5 reshape.36
Async XLA Ops:
  7.2 392.2 %reduce-scatter.4.cloned.1.call-start = ((), (), s32[]{:S(2)}) async-start(), calls=%async_computation.3 | async-start | bytes 37044224
  33.4 1.4 copy-start
  408.0 34.4 %all-to-all-start = ((f32[1,8,28,2368]{3,0,2,1:T(1,128)}), f32[1,8,28,2368]{3,0,2,1:T(1,128)S(1)}, u32[]{:S(2)}, u32[]{:S(2)}) async-start(f32[1,8,28,2368]{3,0,2,1:T(1,128)} %reshape.51), calls=%async_computation | async-start | bytes 4358144 | tf_op jit(solution)/add | solution.py:13
  442.4 36.0 %all-to-all-start.1 = ((f32[1,8,28,2368]{3,0,2,1:T(1,128)}), f32[1,8,28,2368]{3,0,2,1:T(1,128)}, u32[]{:S(2)}, u32[]{:S(2)}) async-start(f32[1,8,28,2368]{3,0,2,1:T(1,128)} %reshape.52), calls=%async_computation.1 | async-start | bytes 4358144 | tf_op jit(solution)/jit(clip)/min | solution.py:20
Sparse Core Ops, SparseCore 0:
  33.5 365.7 reduce-scatter.3
where the time goes:
time: 490 us
  waiting for transfers between devices  414 us (84%)
  matrix products  26.2 us (5%)
  local copies, waits for them, and re-layouts  16.7 us (3%)
  between operations  15.4 us (3%)
  starting transfers between devices  10.7 us (2%)
  other arithmetic  6.19 us (1%)
    unnamed x2, waiting for transfers between devices  364 us
    min x1, waiting for transfers between devices, reference(): ratio = jnp.clip(momentum / (gamma * corrected), -1.0, 1.0)  26.7 us
    dot_general x1, matrix products, reference(): lax.dot_general(acts, cotangent, (((0,), (0,)), ((), ())), preferred_elem...  26.2 us
    add x1, waiting for transfers between devices, reference(): fresh = 0.99 * hessian_ema + 0.01 * estimate  23.7 us
  transfers between devices with their start and end apart: 3, of which 3 were waited for; matrix products, arithmetic and copies ran while one was open for 2% of the time, Pallas kernels for 0%

commit v1 on v0

v1 whole, which is shorter than its diff:
```python
import jax
import jax.numpy as jnp
from jax import lax
from jax.experimental import pallas as pl
from jax.experimental.pallas import tpu as pltpu
from jax.sharding import PartitionSpec as P

TOKENS = 16384
MESH = pl.DeviceIdType.MESH
LANES = 128
WIN = 32

NT = 19
NS = 4
ND = 3
NQ = 3


def kernel(acts, cot_t, hess, mom, gamma_table, layer, steps, fresh_out, ratio_out,
           acts_t, stage, cot, h_in, m_in, tail,
           d_send, d_recv, s_buf, far, direct, relay, q_buf, z_recv, a_send, g_buf, hm_send, hm_buf,
           fresh, ratio,
           ld_sem, cot_sem, st_sem,
           d_ssem, d_rsem, d_free, x_ssem, far_sem, direct_sem, relay_sem,
           z_ssem, z_rsem, a_ssem, a_rsem, h_ssem, h_rsem, o_sem):
    dp = lax.axis_index("dp")
    tn = lax.axis_index("tensor")
    core = lax.rem(dp, 2)
    m = lax.rem(lax.div(dp, 2), 2)
    x = lax.div(dp, 4)
    h = lax.rem(tn, 2)
    y = lax.div(tn, 2)

    def dp_of(x_, m_, core_):
        return (x_ * 2 + m_) * 2 + core_

    partner = (dp_of(x, m, 1 - core), tn)
    right = (dp_of(lax.rem(x + 1, 4), m, core), tn)
    left = (dp_of(lax.rem(x + 3, 4), m, core), tn)
    zpeer = (dp_of(x, 1 - m, core), tn)
    flip_dp = dp_of(x, 1 - m, core)

    acts_ld = [pltpu.make_async_copy(acts.at[:, pl.ds(p * 896, 896)], stage.at[p % 2], ld_sem.at[p]) for p in range(4)]
    acts_ld[0].start()
    acts_ld[1].start()
    cot_ld = [
        pltpu.make_async_copy(cot_t.at[pl.ds(lo, n)], cot.at[pl.ds(pl.multiple_of(lo + 64 * h, 64), n)], cot_sem.at[k])
        for k, (lo, n) in enumerate(((0, 256), (256, 2112)))
    ]
    cot_ld[0].start()
    cot_ld[1].start()
    st_ld = [pltpu.make_async_copy(hess, h_in, st_sem.at[0]), pltpu.make_async_copy(mom, m_in, st_sem.at[1])]
    st_ld[0].start()
    st_ld[1].start()

    barrier = pltpu.get_barrier_semaphore()
    peers = [partner, right, left, zpeer]
    for k in range(1, 8):
        peers.append((dp, lax.rem(tn + k, 8)))
    for k in range(4):
        peers.append((flip_dp, k * 2 + 1 - h))
    for peer in peers:
        pl.semaphore_signal(barrier, inc=1, device_id=peer, device_id_type=MESH)

    cot[pl.ds(pl.multiple_of((1 - h) * 2368, 64), 64), :] = jnp.zeros((64, 1024), jnp.bfloat16)

    for p in range(4):
        acts_ld[p].wait()
        for k in range(7):
            block = stage[p % 2, :, k * LANES:(k + 1) * LANES].T
            row = k * LANES
            done = 0
            while done < LANES:
                which, inside = divmod(row + done, 224)
                size = min(224 - inside, LANES - done)
                dest = (2 * p + which // 2) * 224 + inside
                acts_t[which % 2, dest:dest + size, :] = block[done:done + size]
                done += size
        if p + 2 < 4:
            acts_ld[p + 2].start()
    cot_ld[0].wait()
    cot_ld[1].wait()
    st_ld[0].wait()
    st_ld[1].wait()
    for k, ref in enumerate((h_in, m_in)):
        tail[k] = jnp.concatenate([ref[:, 2304:], jnp.zeros((224, 64), jnp.float32)], axis=1)

    pl.semaphore_wait(barrier, len(peers))

    def product(which, n):
        return lax.dot_general(
            acts_t[which], cot[pl.ds(pl.multiple_of(n * LANES, LANES), LANES), :],
            (((1,), (1,)), ((), ())), preferred_element_type=jnp.float32)

    def remote(src, dst, ssem, rsem, dev):
        return pltpu.make_async_remote_copy(src_ref=src, dst_ref=dst, send_sem=ssem, recv_sem=rsem,
                                            device_id=dev, device_id_type=MESH)

    def d_copy(n):
        return remote(d_send.at[lax.rem(n, 2)], d_recv.at[lax.rem(n, ND)], d_ssem.at[lax.rem(n, 2)],
                      d_rsem.at[lax.rem(n, ND)], partner)

    def blk(n, x_, m_):
        return s_buf.at[lax.rem(n, NS), lax.rem(x + x_, 4) * 2 + m_]

    def x_copies(n):
        s = lax.rem(n, NS)
        return (
            remote(blk(n, 2, 0), far.at[n, 0], x_ssem.at[s, 0], far_sem.at[n, 0], left),
            remote(blk(n, 2, 1), far.at[n, 1], x_ssem.at[s, 1], far_sem.at[n, 1], right),
            remote(blk(n, 1, 0), direct.at[n, 0], x_ssem.at[s, 2], direct_sem.at[n, 0], right),
            remote(blk(n, 3, 1), direct.at[n, 1], x_ssem.at[s, 3], direct_sem.at[n, 1], left),
            remote(blk(n, 3, 0), relay.at[n, 0], x_ssem.at[s, 4], relay_sem.at[n, 0], left),
            remote(blk(n, 1, 1), relay.at[n, 1], x_ssem.at[s, 5], relay_sem.at[n, 1], right),
        )

    def z_copies(n):
        s = lax.rem(n, NQ)
        return (
            remote(q_buf.at[s, 1 - m, :, pl.ds(pl.multiple_of(24 * h, 8), WIN), :], z_recv.at[n, 0],
                   z_ssem.at[s, 0], z_rsem.at[n, 0], zpeer),
            remote(q_buf.at[s, m, :, pl.ds(pl.multiple_of(24 * (1 - h), 8), WIN), :], z_recv.at[n, 1],
                   z_ssem.at[s, 1], z_rsem.at[n, 1], zpeer),
        )

    def a_copies(n):
        s = lax.rem(n, NQ)
        out = []
        for k in range(1, 4):
            to = lax.rem(y + k, 4)
            out.append(remote(a_send.at[s, 0, to], g_buf.at[tn, n], a_ssem.at[s, k - 1], a_rsem.at[n], (dp, to * 2 + h)))
        for k in range(4):
            to = lax.rem(y + k, 4)
            out.append(remote(a_send.at[s, 1, to], g_buf.at[tn, n], a_ssem.at[s, 3 + k], a_rsem.at[n], (flip_dp, to * 2 + 1 - h)))
        return out

    def h_copies(n):
        s = lax.rem(n, NQ)
        out = []
        for k in range(1, 8):
            to = lax.rem(tn + k, 8)
            out.append(remote(hm_send.at[s, :, lax.div(to, 2), pl.ds(pl.multiple_of(24 * lax.rem(to, 2), 8), WIN), :],
                              hm_buf.at[tn, n], h_ssem.at[s, k - 1], h_rsem.at[n], (dp, to)))
        return out

    correction_power = jnp.float32(1.0)
    count = steps[0]
    for bit in range(15):
        correction_power = jnp.where(lax.rem(lax.div(count, 2 ** bit), 2) == 1,
                                     correction_power * jnp.float32(0.99 ** (2 ** bit)), correction_power)
    correction = 1.0 - correction_power
    factor = correction / gamma_table[layer[0]]

    def finish(tile, g, hs, mo):
        new = 0.99 * hs + (0.01 / TOKENS) * (g * g)
        fresh[pl.ds(tile, WIN, stride=148), :] = new
        ratio[pl.ds(tile, WIN, stride=148), :] = jnp.clip(mo * factor / new, -1.0, 1.0)

    lane = lax.broadcasted_iota(jnp.int32, (224, LANES), 1)

    def state_tile(k, ref, n):
        at = lambda i: ref[:, pl.ds(pl.multiple_of(i * LANES, LANES), LANES)]
        here = jnp.where(n < NT - 1, at(jnp.minimum(n, NT - 2)), tail[k])
        before = jnp.where(n > 0, at(jnp.maximum(n - 1, 0)), 0.0)
        moved = jnp.where(lane < 64, pltpu.roll(before, 64, 1), pltpu.roll(here, 64, 1))
        return jnp.where(h == 0, here, moved)

    def body(t, carry):
        n = t

        @pl.when(n < NT)
        def _():
            s = lax.rem(n, NQ)

            @pl.when(n >= NQ)
            def _():
                for c in h_copies(n - NQ):
                    c.wait_send()
            hm_send[s, 0] = state_tile(0, h_in, n).reshape(4, 56, LANES)
            hm_send[s, 1] = state_tile(1, m_in, n).reshape(4, 56, LANES)
            hm_buf[tn, n] = hm_send[s, :, y, pl.ds(pl.multiple_of(24 * h, 8), WIN), :]
            for c in h_copies(n):
                c.start()

            @pl.when(n >= 2)
            def _():
                d_copy(n - 2).wait_send()
            d_send[lax.rem(n, 2)] = product(1 - core, n)

            @pl.when(n >= ND)
            def _():
                pl.semaphore_wait(d_free, 1)
            d_copy(n).start()

        n1 = t - 1

        @pl.when(jnp.logical_and(n1 >= 0, n1 < NT))
        def _():
            @pl.when(n1 >= NS)
            def _():
                for c in x_copies(n1 - NS):
                    c.wait_send()
            own = product(core, n1)
            d_copy(n1).wait_recv()
            s_buf[lax.rem(n1, NS)] = (own + d_recv[lax.rem(n1, ND)]).reshape(8, 224, LANES)

            @pl.when(n1 < NT - ND)
            def _():
                pl.semaphore_signal(d_free, inc=1, device_id=partner, device_id_type=MESH)
            for c in x_copies(n1)[:4]:
                c.start()

        n2 = t - 2

        @pl.when(jnp.logical_and(n2 >= 0, n2 < NT))
        def _():
            cs = x_copies(n2)
            for half, c, at in ((0, cs[4], 3), (1, cs[5], 1)):
                cs[half].wait_recv()
                b = blk(n2, at, half)
                b[...] = b[...] + far[n2, half]
                c.start()

        n3 = t - 3

        @pl.when(jnp.logical_and(n3 >= 0, n3 < NT))
        def _():
            @pl.when(n3 >= NQ)
            def _():
                for c in z_copies(n3 - NQ):
                    c.wait_send()
            cs = x_copies(n3)
            for half in range(2):
                cs[2 + half].wait_recv()
                cs[4 + half].wait_recv()
                total = blk(n3, 0, half)[...] + direct[n3, half] + relay[n3, half]
                q_buf[lax.rem(n3, NQ), half] = total.reshape(4, 56, LANES)
            for c in z_copies(n3):
                c.start()

        n4 = t - 4

        @pl.when(jnp.logical_and(n4 >= 0, n4 < NT))
        def _():
            s = lax.rem(n4, NQ)

            @pl.when(n4 >= NQ)
            def _():
                for c in a_copies(n4 - NQ):
                    c.wait_send()
            for c in z_copies(n4):
                c.wait_recv()
            a_send[s, 0] = q_buf[s, m, :, pl.ds(pl.multiple_of(24 * h, 8), WIN), :] + z_recv[n4, 0]
            a_send[s, 1] = q_buf[s, 1 - m, :, pl.ds(pl.multiple_of(24 * (1 - h), 8), WIN), :] + z_recv[n4, 1]
            g_buf[tn, n4] = a_send[s, 0, y]
            for c in a_copies(n4):
                c.start()

        n5 = t - 5

        @pl.when(n5 >= 0)
        def _():
            remote(g_buf.at[pl.ds(0, 7), n5], g_buf.at[pl.ds(0, 7), n5], a_ssem.at[0, 0], a_rsem.at[n5], partner).wait_recv()
            remote(hm_buf.at[pl.ds(0, 7), n5], hm_buf.at[pl.ds(0, 7), n5], h_ssem.at[0, 0], h_rsem.at[n5], partner).wait_recv()

            @pl.when(n5 < NT - 1)
            def _():
                for j in range(0, 8, 2):
                    finish(37 * (j // 2) + n5, g_buf[j, n5], hm_buf[j, n5, 0], hm_buf[j, n5, 1])

            @pl.when(n5 >= 1)
            def _():
                for j in range(1, 8, 2):
                    finish(37 * (j // 2) + 18 + n5, g_buf[j, n5], hm_buf[j, n5, 0], hm_buf[j, n5, 1])
        return carry

    lax.fori_loop(0, NT + 5, body, 0)

    for j in range(0, 8, 2):
        finish(37 * (j // 2) + 18, g_buf[j, NT - 1] + g_buf[j + 1, 0],
               hm_buf[j, NT - 1, 0] + hm_buf[j + 1, 0, 0], hm_buf[j, NT - 1, 1] + hm_buf[j + 1, 0, 1])
    first = pl.multiple_of(4 * 148 * h, 8)
    outs = [pltpu.make_async_copy(fresh.at[pl.ds(first, 4144), :], fresh_out, o_sem.at[0]),
            pltpu.make_async_copy(ratio.at[pl.ds(first, 4144), :], ratio_out, o_sem.at[1])]
    for c in outs:
        c.start()

    for n in range(NT - NS, NT):
        for c in x_copies(n):
            c.wait_send()
    for n in range(NT - NQ, NT):
        for c in z_copies(n):
            c.wait_send()
        for c in a_copies(n):
            c.wait_send()
        for c in h_copies(n):
            c.wait_send()
    for n in range(NT - 2, NT):
        d_copy(n).wait_send()
    for c in outs:
        c.wait()


def local(acts, cot, hess, mom, gamma_table, layer, steps):
    f32, bf16 = jnp.float32, jnp.bfloat16
    dma, vmem = pltpu.SemaphoreType.DMA, pltpu.VMEM
    anyspec = pl.BlockSpec(memory_space=pl.ANY)
    smem = pl.BlockSpec(memory_space=pltpu.SMEM)
    out = jax.ShapeDtypeStruct((4144, LANES), f32)
    fresh, ratio = pl.pallas_call(
        kernel,
        out_shape=(out, out),
        in_specs=[anyspec] * 4 + [smem] * 3,
        out_specs=(anyspec, anyspec),
        scratch_shapes=[
            vmem((2, 1792, 1024), bf16), vmem((2, 1024, 896), bf16), vmem((NT * LANES, 1024), bf16),
            vmem((224, 2368), f32), vmem((224, 2368), f32), vmem((2, 224, LANES), f32),
            vmem((2, 1792, LANES), f32), vmem((ND, 1792, LANES), f32), vmem((NS, 8, 224, LANES), f32),
            vmem((NT, 2, 224, LANES), f32), vmem((NT, 2, 224, LANES), f32), vmem((NT, 2, 224, LANES), f32),
            vmem((NQ, 2, 4, 56, LANES), f32), vmem((NT, 2, 4, WIN, LANES), f32), vmem((NQ, 2, 4, WIN, LANES), f32),
            vmem((8, NT, WIN, LANES), f32), vmem((NQ, 2, 4, 56, LANES), f32), vmem((8, NT, 2, WIN, LANES), f32),
            vmem((WIN * 148, LANES), f32), vmem((WIN * 148, LANES), f32),
            dma((4,)), dma((2,)), dma((2,)),
            dma((2,)), dma((ND,)), pltpu.SemaphoreType.REGULAR, dma((NS, 6)), dma((NT, 2)), dma((NT, 2)), dma((NT, 2)),
            dma((NQ, 2)), dma((NT, 2)), dma((NQ, 7)), dma((NT,)), dma((NQ, 7)), dma((NT,)), dma((2,)),
        ],
        compiler_params=pltpu.CompilerParams(collective_id=0, has_side_effects=True, vmem_limit_bytes=67043328),
    )(acts, cot.T, hess, mom, gamma_table, layer, steps)
    return fresh.reshape(-1), ratio.reshape(-1)


def solution(mesh):
    return jax.shard_map(
        local, mesh=mesh,
        in_specs=(P("dp", None), P("dp", "tensor"), P("dp", "tensor"), P("dp", "tensor"), P(None), P(None), P(None)),
        out_specs=(P(("dp", "tensor")), P(("dp", "tensor"))),
        check_vma=False)
```

time: 490 us -> 181 us (0.37)
  waiting for transfers between devices: 414 us -> 0 us
  Pallas kernels: 0 us -> 174 us
  matrix products: 26.2 us -> 0 us
  between operations: 15.4 us -> 1.94 us
  local copies, waits for them, and re-layouts: 16.7 us -> 4.68 us
  starting transfers between devices: 10.7 us -> 0 us
  other arithmetic: 6.19 us -> 0 us
    unnamed x2 -> x0, waiting for transfers between devices: 364 us -> none
    pallas_call x0 -> x1, Pallas kernels: none -> 174 us  [local(): pl.pallas_call(kernel, out_shape=(out, out), in_specs=[anyspec] * 4 + [sm...]
    min x1 -> x0, waiting for transfers between devices: 26.7 us -> none  [reference(): ratio = jnp.clip(momentum / (gamma * corrected), -1.0, 1.0)]
    dot_general x1 -> x0, matrix products: 26.2 us -> none  [reference(): lax.dot_general(acts, cotangent, (((0,), (0,)), ((), ())), preferred_elem...]
    add x1 -> x0, waiting for transfers between devices: 23.7 us -> none  [reference(): fresh = 0.99 * hessian_ema + 0.01 * estimate]
    add x1 -> x0, starting transfers between devices: 6.3 us -> none  [reference(): fresh = 0.99 * hessian_ema + 0.01 * estimate]
    min x2 -> x0, local copies, waits for them, and re-layouts: 6.19 us -> none  [reference(): ratio = jnp.clip(momentum / (gamma * corrected), -1.0, 1.0)]
    reshape x2 -> x0, local copies, waits for them, and re-layouts: 5.88 us -> none  [reference(): return (fresh.reshape(-1), ratio.reshape(-1))]
  transfers between devices with their start and end apart: 3 -> 0, of which waited for: 3 -> 0; matrix products, arithmetic and copies ran while one was open for 2% -> 0% of each run, Pallas kernels for 0% -> 0%
where the time goes in v1:
time: 181 us; the launch traced here: 180 us
  Pallas kernels  174 us (96%)
  local copies, waits for them, and re-layouts  4.68 us (3%)
  between operations  1.94 us (1%)
    pallas_call x1, Pallas kernels, local(): pl.pallas_call(kernel, out_shape=(out, out), in_specs=[anyspec] * 4 + [sm...  174 us
    unnamed x4, local copies, waits for them, and re-layouts  4.68 us

profile of v1, /device:TPU:1, one launch (start us, length us, event | category | flops | bytes accessed | tf_op | source)
XLA Modules:
  0.0 180.5 jit_solution(4991860925494870905)
XLA Ops:
  1.9 173.8 %shard_map.86 = (f32[4144,128]{1,0:T(8,128)}, f32[4144,128]{1,0:T(8,128)}) custom-call(bf16[1024,3584]{1,0:T(8,128)(2,1)} %acts.1, bf16[2368,1024]{1,0:T(8,128)(2,1)} %bitcast.3, f32[224,2368]{1,0:T(8,128)} %hess.1, f32[224,2368]{1,0:T(8,128)} %mom.1, f32[28]{0:T(128)} %gamma_table.1, s32[1]{0:T(128)S(6)} %copy.11.layer, s32[1]{0:T(128)S(6)} %copy.12.steps), custom_call_target="tpu_custom_call" | custom-call | tf_op jit(solution)/shard_map/pallas_call | solution.py:310
  175.8 0.0 copy-start
  175.8 3.2 %copy.13 = f32[530432]{0:T(1024)} copy(f32[530432]{0:T(1024)} %bitcast.5) | data formatting | bytes 4243456
  179.0 0.0 copy-done
  179.0 1.5 copy.14
Async XLA Ops:
  175.8 3.2 %copy-start = (f32[4144,128]{1,0:T(8,128)S(1)}, f32[4144,128]{1,0:T(8,128)}, u32[]{:S(2)}) copy-start(f32[4144,128]{1,0:T(8,128)} %get-tuple-element.5) | copy-start | bytes 6365188

commit v2 on v0

v2 whole, which is shorter than its diff:
```python
import jax
import jax.numpy as jnp
from jax import lax
from jax.experimental import pallas as pl
from jax.experimental.pallas import tpu as pltpu
from jax.sharding import PartitionSpec as P

TOKENS = 16384
MESH = pl.DeviceIdType.MESH
LANES = 128
WIN = 32

NT = 19
NZ = 3
NX = NT - NZ
HALF = NX - 1
NS = 4
ND = 3
NQ = 4
NH = 6


def kernel(acts, cot_t, hess, mom, gamma_table, layer, steps, fresh, ratio,
           acts_t, stage, cot, h_in, m_in, tail,
           d_send, d_recv, s_buf, far, direct, relay, q_buf, z_recv, a_send, g_buf, hm_send, hm_buf,
           zs, zf, far_z, direct_z, relay_z, az,
           ld_sem, cot_sem, st_sem,
           d0_ssem, d0_rsem, d_ssem, d_rsem, d_free, x_ssem, far_sem, direct_sem, relay_sem,
           z_ssem, z_rsem, a_ssem, a_rsem, h_ssem, h_rsem, zf_ssem, zf_rsem, xz_ssem, az_ssem):
    dp = lax.axis_index("dp")
    tn = lax.axis_index("tensor")
    core = lax.rem(dp, 2)
    m = lax.rem(lax.div(dp, 2), 2)
    x = lax.div(dp, 4)
    h = lax.rem(tn, 2)
    y = lax.div(tn, 2)

    def dp_of(x_, m_, core_):
        return (x_ * 2 + m_) * 2 + core_

    def x_at(k):
        return lax.rem(x + k, 4)

    partner = (dp_of(x, m, 1 - core), tn)
    right = (dp_of(x_at(1), m, core), tn)
    left = (dp_of(x_at(3), m, core), tn)
    flip_dp = dp_of(x, 1 - m, core)
    zpeer = (flip_dp, tn)

    barrier = pltpu.get_barrier_semaphore()
    peers = []
    for k in (2, 1, 3, 0):
        if k:
            peers.append((dp, lax.rem(y + k, 4) * 2 + h))
        peers.append((dp, lax.rem(y + k, 4) * 2 + 1 - h))
        peers.append((flip_dp, lax.rem(y + k, 4) * 2 + 1 - h))
    peers += [zpeer, left, right, partner]
    for peer in peers:
        pl.semaphore_signal(barrier, inc=1, device_id=peer, device_id_type=MESH)

    order = [x_at(2), x_at(1), x_at(3), x]
    cot_ld = [
        pltpu.make_async_copy(cot_t.at[pl.ds(lo, n)], cot.at[pl.ds(pl.multiple_of(lo + 64 * h, 64), n)], cot_sem.at[k])
        for k, (lo, n) in enumerate(((0, 192), (192, 2176)))
    ]
    acts_ld = [pltpu.make_async_copy(acts.at[:, pl.ds(pl.multiple_of(p * 896, LANES), 896)], stage.at[k % 2], ld_sem.at[k])
               for k, p in enumerate(order)]
    st_ld = [pltpu.make_async_copy(hess, h_in, st_sem.at[0]), pltpu.make_async_copy(mom, m_in, st_sem.at[1])]
    acts_ld[0].start()
    cot_ld[0].start()
    acts_ld[1].start()

    cot[pl.ds(pl.multiple_of((1 - h) * 2368, 64), 64), :] = jnp.zeros((64, 1024), jnp.bfloat16)

    def remote(src, dst, ssem, rsem, dev):
        return pltpu.make_async_remote_copy(src_ref=src, dst_ref=dst, send_sem=ssem, recv_sem=rsem,
                                            device_id=dev, device_id_type=MESH)

    def tile_of(n, h_):
        return jnp.where(n == HALF, (NT - 1) * (1 - h_), n + h_ - (n > HALF).astype(jnp.int32))

    def matmul(rows, n):
        return lax.dot_general(
            rows, cot[pl.ds(pl.multiple_of(tile_of(n, h) * LANES, LANES), LANES), :],
            (((1,), (1,)), ((), ())), preferred_element_type=jnp.float32)

    def product(which, n):
        return matmul(acts_t[which].reshape(1792, 1024), n).reshape(4, 448, LANES)

    def q_of_x(n):
        return n + jnp.minimum(lax.div(jnp.maximum(n - 2, 0), 4), NZ)

    def q_of_z(i):
        return 5 * i + 6

    def d0_copy(k):
        return remote(d_send.at[0, order[k]], d_recv.at[0, order[k]], d0_ssem.at[k], d0_rsem.at[k], partner)

    def d_copy(q):
        return remote(d_send.at[lax.rem(q, 2)], d_recv.at[lax.rem(q, ND)], d_ssem.at[lax.rem(q, 2)],
                      d_rsem.at[lax.rem(q, ND)], partner)

    def x_set(at, half_of, far_, direct_, relay_, ssem, fsem, dsem, rsem):
        return (
            remote(half_of(at(2), 0), far_.at[0], ssem.at[0], fsem.at[0], left),
            remote(half_of(at(2), 1), far_.at[1], ssem.at[1], fsem.at[1], right),
            remote(half_of(at(1), 0), direct_.at[0], ssem.at[2], dsem.at[0], right),
            remote(half_of(at(3), 1), direct_.at[1], ssem.at[3], dsem.at[1], left),
            remote(half_of(at(3), 0), relay_.at[0], ssem.at[4], rsem.at[0], left),
            remote(half_of(at(1), 1), relay_.at[1], ssem.at[5], rsem.at[1], right),
        )

    def blk(n, k, half):
        return s_buf.at[lax.rem(n, NS), x_at(k), half]

    def x_copies(n):
        return x_set(lambda k: s_buf.at[lax.rem(n, NS), x_at(k)], lambda r, half: r.at[half],
                     far.at[n], direct.at[n], relay.at[n], x_ssem.at[lax.rem(n, NS)],
                     far_sem.at[n], direct_sem.at[n], relay_sem.at[n])

    def half_copies():
        short = pl.ds(0, 112)
        return x_set(lambda k: s_buf.at[HALF % NS, x_at(k)], lambda r, half: r.at[half, short, :],
                     far.at[HALF, :, short, :], direct.at[HALF, :, short, :], relay.at[HALF, :, short, :],
                     x_ssem.at[HALF % NS], far_sem.at[HALF], direct_sem.at[HALF], relay_sem.at[HALF])

    def zblk(i, k, half):
        return zs.at[i, x_at(k), m, pl.ds(112 * half, 112), :]

    def xz_copies(i):
        return x_set(lambda k: zs.at[i, x_at(k), m], lambda r, half: r.at[pl.ds(112 * half, 112), :],
                     far_z.at[i], direct_z.at[i], relay_z.at[i], xz_ssem.at[i],
                     far_sem.at[NX + i], direct_sem.at[NX + i], relay_sem.at[NX + i])

    def zf_copy(i, k):
        return remote(zs.at[i, k, 1 - m], zf.at[i, k], zf_ssem.at[i, k], zf_rsem.at[i, k], zpeer)

    def z_copies(n):
        s = lax.rem(n, NQ)
        return (remote(q_buf.at[s, 1 - m, h], z_recv.at[n, 0], z_ssem.at[s, 0], z_rsem.at[n, 0], zpeer),
                remote(q_buf.at[s, m, 1 - h], z_recv.at[n, 1], z_ssem.at[s, 1], z_rsem.at[n, 1], zpeer))

    def window(to):
        return pl.ds(pl.multiple_of(28 * to - 4 * lax.rem(to, 2), 8), WIN)

    def a_copies(n):
        s = lax.rem(n, NQ)
        out = []
        for k in range(1, 4):
            to = lax.rem(y + k, 4)
            out.append(remote(a_send.at[s, 0, window(to), :], g_buf.at[tn, n], a_ssem.at[s, k - 1], a_rsem.at[n], (dp, to * 2 + h)))
        for k in range(4):
            to = lax.rem(y + k, 4)
            out.append(remote(a_send.at[s, 1, window(to), :], g_buf.at[tn, n], a_ssem.at[s, 3 + k], a_rsem.at[n], (flip_dp, to * 2 + 1 - h)))
        return out

    def az_copies(i):
        out = []
        for k in range(1, 8):
            to = lax.rem(tn + k, 8)
            out.append(remote(az.at[i, lax.rem(to, 2), window(lax.div(to, 2)), :], g_buf.at[tn, NX + i],
                              az_ssem.at[i, k - 1], a_rsem.at[NX + i], (dp, to)))
        return out

    def h_copies(n):
        s = lax.rem(n, NH)
        out = []
        for k in range(1, 8):
            to = lax.rem(tn + k, 8)
            out.append(remote(hm_send.at[s, :, lax.div(to, 2), pl.ds(pl.multiple_of(24 * lax.rem(to, 2), 8), WIN), :],
                              hm_buf.at[tn, n], h_ssem.at[s, k - 1], h_rsem.at[n], (dp, to)))
        return out

    def turn(k):
        for i in range(7):
            block = stage[k % 2, :, i * LANES:(i + 1) * LANES].T
            done = 0
            while done < LANES:
                which, inside = divmod(i * LANES + done, 224)
                size = min(224 - inside, LANES - done)
                dest = (which // 2) * 224 + inside
                acts_t[which % 2, order[k], dest:dest + size, :] = block[done:done + size]
                done += size

    def own_piece(k):
        p = order[k]
        own = matmul(acts_t[core, p], jnp.int32(0))
        d0_copy(k).wait_recv()
        s_buf[0, p] = (own + d_recv[0, p]).reshape(2, 224, LANES)

    first = x_copies(0)
    for k in range(4):
        acts_ld[k].wait()
        turn(k)
        if k < 2:
            acts_ld[k + 2].start()
        if k == 0:
            cot_ld[1].start()
            cot_ld[0].wait()
        if k == 1:
            st_ld[0].start()
            st_ld[1].start()
        d_send[0, order[k]] = matmul(acts_t[1 - core, order[k]], jnp.int32(0))
        if k == 0:
            pl.semaphore_wait(barrier, len(peers))
        d0_copy(k).start()
        if k == 1:
            own_piece(0)
            first[0].start()
            first[1].start()
        if k == 2:
            own_piece(1)
            first[2].start()
    own_piece(2)
    first[3].start()
    own_piece(3)
    pl.semaphore_signal(d_free, inc=1, device_id=partner, device_id_type=MESH)

    def pass_on(cs, at_half, far_):
        for half, at in ((0, 3), (1, 1)):
            cs[half].wait_recv()
            b = at_half(at, half)
            b[...] = b[...] + far_[half]
            cs[4 + half].start()

    def send_partial(n, q):
        @pl.when(q >= 3)
        def _():
            d_copy(q - 2).wait_send()
        d_send[lax.rem(q, 2)] = product(1 - core, n)

        @pl.when(q >= ND)
        def _():
            pl.semaphore_wait(d_free, 1)
        d_copy(q).start()

    cot_ld[1].wait()
    send_partial(jnp.int32(1), jnp.int32(1))
    pass_on(first, lambda k, half: blk(0, k, half), far.at[0])
    for k in range(4):
        d0_copy(k).wait_send()
    st_ld[0].wait()
    st_ld[1].wait()
    for k, ref in enumerate((h_in, m_in)):
        tail[k] = jnp.concatenate([ref[:, 2304:], jnp.zeros((224, 64), jnp.float32)], axis=1)

    correction_power = jnp.float32(1.0)
    count = steps[0]
    for bit in range(15):
        correction_power = jnp.where(lax.rem(lax.div(count, 2 ** bit), 2) == 1,
                                     correction_power * jnp.float32(0.99 ** (2 ** bit)), correction_power)
    correction = 1.0 - correction_power
    factor = correction / gamma_table[layer[0]]
    y_odd = lax.rem(y, 2) == 1

    def trim(v, odd):
        return jnp.where(odd, v[4:], v[:28])

    def finish(tile, g, hs, mo):
        g, hs, mo = trim(g, y_odd), trim(hs, h == 1), trim(mo, h == 1)
        new = 0.99 * hs + (0.01 / TOKENS) * (g * g)
        fresh[pl.ds(tile, 28, stride=148), :] = new
        ratio[pl.ds(tile, 28, stride=148), :] = jnp.clip(mo * factor / new, -1.0, 1.0)

    lane = lax.broadcasted_iota(jnp.int32, (224, LANES), 1)

    def state_tile(k, ref, n):
        at = lambda i: ref[:, pl.ds(pl.multiple_of(i * LANES, LANES), LANES)]
        here = jnp.where(n < NT - 1, at(jnp.minimum(n, NT - 2)), tail[k])
        before = jnp.where(n > 0, at(jnp.maximum(n - 1, 0)), 0.0)
        moved = jnp.where(lane < 64, pltpu.roll(before, 64, 1), pltpu.roll(here, 64, 1))
        return jnp.where(h == 0, here, moved)

    low = lane[:112] < 64

    def pack(v):
        a, b = v[:112], v[112:]
        return jnp.where(h == 0, a + pltpu.roll(b, 64, 1), pltpu.roll(a, 64, 1) + b)

    def unpack(v):
        w = pltpu.roll(v, 64, 1)
        a = jnp.where(h == 0, jnp.where(low, v, 0.0), jnp.where(low, 0.0, w))
        b = jnp.where(h == 0, jnp.where(low, w, 0.0), jnp.where(low, 0.0, v))
        return jnp.concatenate([a, b], axis=0)

    def states_before(t):
        n = jnp.where(t <= 3, 3 * t - 3, jnp.where(t <= 5, 2 * t, t + 5))
        return jnp.minimum(n, NT)

    def state_step(n, carry):
        s = lax.rem(n, NH)

        @pl.when(n >= NH)
        def _():
            for c in h_copies(n - NH):
                c.wait_send()
        hm_send[s, 0] = state_tile(0, h_in, tile_of(n, h)).reshape(4, 56, LANES)
        hm_send[s, 1] = state_tile(1, m_in, tile_of(n, h)).reshape(4, 56, LANES)
        hm_buf[tn, n] = hm_send[s, :, y, pl.ds(pl.multiple_of(24 * h, 8), WIN), :]
        for c in h_copies(n):
            c.start()
        return carry

    def by_z_hi(dst, v):
        for y_ in range(4):
            for z_ in range(2):
                dst[z_, 28 * y_:28 * y_ + 28, :] = v[56 * y_ + 28 * z_:56 * y_ + 28 * z_ + 28]

    def own_sum(n, q):
        own = product(core, n)
        d_copy(q).wait_recv()
        total = (own + d_recv[lax.rem(q, ND)]).reshape(4, 2, 224, LANES)

        return total

    def free(q):
        @pl.when(q < NT - ND)
        def _():
            pl.semaphore_signal(d_free, inc=1, device_id=partner, device_id_type=MESH)

    def within(n, lo, hi):
        return pl.when(jnp.logical_and(n >= lo, n < hi))

    def body(t, carry):
        @within(t, 1, NX)
        def _():
            q = q_of_x(t)

            @pl.when(t >= NS)
            def _():
                for c in x_copies(t - NS):
                    c.wait_send()

            @pl.when(t < HALF)
            def _():
                s_buf[lax.rem(t, NS)] = own_sum(t, q)
                for c in x_copies(t)[:4]:
                    c.start()

            @pl.when(t == HALF)
            def _():
                total = own_sum(t, q)
                for k in range(4):
                    for half in range(2):
                        s_buf[HALF % NS, k, half, pl.ds(0, 112), :] = pack(total[k, half])
                for c in half_copies()[:4]:
                    c.start()
            free(q)

        @pl.when(t + 1 < NX)
        def _():
            send_partial(t + 1, q_of_x(t + 1))

        zi = lax.div(t - 5, 4)

        @pl.when(jnp.logical_and(lax.rem(t, 4) == 1, jnp.logical_and(t >= 5, t <= 4 * NZ + 1)))
        def _():
            q = q_of_z(zi)
            zs[zi] = own_sum(NX + zi, q)
            free(q)

        @within(t, 5, 5 + 4 * NZ)
        def _():
            zf_copy(zi, lax.rem(t - 5 + x + 2, 4)).start()

        @within(t, NX, NT)
        def _():
            i = t - NX
            cs = xz_copies(i)
            for k, go in ((2, (0, 1)), (1, (2,)), (3, (3,)), (0, ())):
                zf_copy(i, x_at(k)).wait_recv()
                zs[i, x_at(k), m] = zs[i, x_at(k), m] + zf[i, x_at(k)]
                for g in go:
                    cs[g].start()

        u2 = t - 1

        @within(u2, 1, HALF)
        def _():
            pass_on(x_copies(u2), lambda k, half: blk(u2, k, half), far.at[u2])

        @pl.when(u2 == HALF)
        def _():
            short = pl.ds(0, 112)
            pass_on(half_copies(), lambda k, half: s_buf.at[HALF % NS, x_at(k), half, short, :], far.at[HALF, :, short, :])

        @within(u2, NX, NT)
        def _():
            i = u2 - NX
            pass_on(xz_copies(i), lambda k, half: zblk(i, k, half), far_z.at[i])

        @pl.when(jnp.logical_and(lax.rem(t, 4) == 0, jnp.logical_and(t >= 4, t <= 4 * NZ)))
        def _():
            send_partial(NX + lax.div(t - 4, 4), q_of_z(lax.div(t - 4, 4)))

        lax.fori_loop(states_before(t), states_before(t + 1), state_step, 0)

        u3 = t - 3

        @within(u3, 0, NX)
        def _():
            @pl.when(u3 >= NQ)
            def _():
                for c in z_copies(u3 - NQ):
                    c.wait_send()
            s = lax.rem(u3, NQ)

            @pl.when(u3 < HALF)
            def _():
                cs = x_copies(u3)
                for half in range(2):
                    cs[2 + half].wait_recv()
                    cs[4 + half].wait_recv()
                    by_z_hi(q_buf.at[s, half], blk(u3, 0, half)[...] + direct[u3, half] + relay[u3, half])

            @pl.when(u3 == HALF)
            def _():
                cs = half_copies()
                for half in range(2):
                    cs[2 + half].wait_recv()
                    cs[4 + half].wait_recv()
                    total = s_buf[HALF % NS, x, half, :112] + direct[HALF, half, :112] + relay[HALF, half, :112]
                    by_z_hi(q_buf.at[s, half], unpack(total))
            for c in z_copies(u3):
                c.start()

        @within(u3, NX, NT)
        def _():
            i = u3 - NX
            cs = xz_copies(i)
            halves = []
            for half in range(2):
                cs[2 + half].wait_recv()
                cs[4 + half].wait_recv()
                halves.append(zblk(i, 0, half)[...] + direct_z[i, half] + relay_z[i, half])
            by_z_hi(az.at[i], jnp.concatenate(halves, axis=0))
            g_buf[tn, NX + i] = az[i, h, window(y), :]
            for c in az_copies(i):
                c.start()

        u4 = t - 5

        @within(u4, 0, NX)
        def _():
            s = lax.rem(u4, NQ)

            @pl.when(u4 >= NQ)
            def _():
                for c in a_copies(u4 - NQ):
                    c.wait_send()
            for c in z_copies(u4):
                c.wait_recv()
            a_send[s, 0] = q_buf[s, m, h] + z_recv[u4, 0]
            a_send[s, 1] = q_buf[s, 1 - m, 1 - h] + z_recv[u4, 1]
            g_buf[tn, u4] = a_send[s, 0, window(y), :]
            for c in a_copies(u4):
                c.start()

        u5 = t - 7

        @pl.when(u5 >= 0)
        def _():
            remote(g_buf.at[pl.ds(0, 7), u5], g_buf.at[pl.ds(0, 7), u5], a_ssem.at[0, 0], a_rsem.at[u5], partner).wait_recv()
            remote(hm_buf.at[pl.ds(0, 7), u5], hm_buf.at[pl.ds(0, 7), u5], h_ssem.at[0, 0], h_rsem.at[u5], partner).wait_recv()

            @pl.when(u5 != HALF)
            def _():
                for j in range(8):
                    finish(37 * (j // 2) + 18 * (j % 2) + tile_of(u5, j % 2), g_buf[j, u5], hm_buf[j, u5, 0], hm_buf[j, u5, 1])

            @pl.when(u5 == HALF)
            def _():
                for j in range(0, 8, 2):
                    finish(37 * (j // 2) + 18, *(a + b for a, b in (
                        (g_buf[j, HALF], g_buf[j + 1, HALF]),
                        (hm_buf[j, HALF, 0], hm_buf[j + 1, HALF, 0]), (hm_buf[j, HALF, 1], hm_buf[j + 1, HALF, 1]))))
        return carry

    lax.fori_loop(1, NT + 7, body, 0)

    for n in range(NX - NS, NX):
        for c in half_copies() if n == HALF else x_copies(n):
            c.wait_send()
    for n in range(NX - NQ, NX):
        for c in z_copies(n) + tuple(a_copies(n)):
            c.wait_send()
    for n in range(NT - NH, NT):
        for c in h_copies(n):
            c.wait_send()
    for i in range(NZ):
        for k in range(4):
            zf_copy(i, k).wait_send()
        for c in xz_copies(i) + tuple(az_copies(i)):
            c.wait_send()
    for q in range(NT - 2, NT):
        d_copy(q).wait_send()


def local(acts, cot, hess, mom, gamma_table, layer, steps):
    f32, bf16 = jnp.float32, jnp.bfloat16
    dma, vmem = pltpu.SemaphoreType.DMA, pltpu.VMEM
    anyspec = pl.BlockSpec(memory_space=pl.ANY)
    smem = pl.BlockSpec(memory_space=pltpu.SMEM)
    out = pltpu.VMEM((4144, LANES), f32)
    fresh, ratio = pl.pallas_call(
        kernel,
        out_shape=(out, out),
        in_specs=[anyspec] * 4 + [smem] * 3,
        out_specs=(pl.BlockSpec(memory_space=pltpu.VMEM),) * 2,
        scratch_shapes=[
            vmem((2, 4, 448, 1024), bf16), vmem((2, 1024, 896), bf16), vmem((NT * LANES, 1024), bf16),
            vmem((224, 2368), f32), vmem((224, 2368), f32), vmem((2, 224, LANES), f32),
            vmem((2, 4, 448, LANES), f32), vmem((ND, 4, 448, LANES), f32), vmem((NS, 4, 2, 224, LANES), f32),
            vmem((NX, 2, 224, LANES), f32), vmem((NX, 2, 224, LANES), f32), vmem((NX, 2, 224, LANES), f32),
            vmem((NQ, 2, 2, 112, LANES), f32), vmem((NX, 2, 112, LANES), f32), vmem((NQ, 2, 112, LANES), f32),
            vmem((8, NT, WIN, LANES), f32), vmem((NH, 2, 4, 56, LANES), f32), vmem((8, NT, 2, WIN, LANES), f32),
            vmem((NZ, 4, 2, 224, LANES), f32), vmem((NZ, 4, 224, LANES), f32),
            vmem((NZ, 2, 112, LANES), f32), vmem((NZ, 2, 112, LANES), f32), vmem((NZ, 2, 112, LANES), f32),
            vmem((NZ, 2, 112, LANES), f32),
            dma((4,)), dma((2,)), dma((2,)),
            dma((4,)), dma((4,)), dma((2,)), dma((ND,)), pltpu.SemaphoreType.REGULAR,
            dma((NS, 6)), dma((NT, 2)), dma((NT, 2)), dma((NT, 2)),
            dma((NQ, 2)), dma((NX, 2)), dma((NQ, 7)), dma((NT,)), dma((NH, 7)), dma((NT,)),
            dma((NZ, 4)), dma((NZ, 4)), dma((NZ, 6)), dma((NZ, 7)),
        ],
        compiler_params=pltpu.CompilerParams(collective_id=0, has_side_effects=True, vmem_limit_bytes=62500000),
    )(acts, cot.T, hess, mom, gamma_table, layer, steps)
    return fresh.reshape(-1), ratio.reshape(-1)


def solution(mesh):
    return jax.shard_map(
        local, mesh=mesh,
        in_specs=(P("dp", None), P("dp", "tensor"), P("dp", "tensor"), P("dp", "tensor"), P(None), P(None), P(None)),
        out_specs=(P(("dp", "tensor")), P(("dp", "tensor"))),
        check_vma=False)
```

time: 490 us -> 162 us (0.33)
  waiting for transfers between devices: 414 us -> 0 us
  Pallas kernels: 0 us -> 156 us
  matrix products: 26.2 us -> 0 us
  local copies, waits for them, and re-layouts: 16.7 us -> 2.93 us
  between operations: 15.4 us -> 1.93 us
  starting transfers between devices: 10.7 us -> 0 us
  other arithmetic: 6.19 us -> 0 us
    unnamed x2 -> x0, waiting for transfers between devices: 364 us -> none
    pallas_call x0 -> x1, Pallas kernels: none -> 156 us  [local(): pl.pallas_call(kernel, out_shape=(out, out), in_specs=[anyspec] * 4 + [sm...]
    min x1 -> x0, waiting for transfers between devices: 26.7 us -> none  [reference(): ratio = jnp.clip(momentum / (gamma * corrected), -1.0, 1.0)]
    dot_general x1 -> x0, matrix products: 26.2 us -> none  [reference(): lax.dot_general(acts, cotangent, (((0,), (0,)), ((), ())), preferred_elem...]
    add x1 -> x0, waiting for transfers between devices: 23.7 us -> none  [reference(): fresh = 0.99 * hessian_ema + 0.01 * estimate]
    add x1 -> x0, starting transfers between devices: 6.3 us -> none  [reference(): fresh = 0.99 * hessian_ema + 0.01 * estimate]
    min x2 -> x0, local copies, waits for them, and re-layouts: 6.19 us -> none  [reference(): ratio = jnp.clip(momentum / (gamma * corrected), -1.0, 1.0)]
    reshape x2 -> x0, local copies, waits for them, and re-layouts: 5.88 us -> none  [reference(): return (fresh.reshape(-1), ratio.reshape(-1))]
  transfers between devices with their start and end apart: 3 -> 0, of which waited for: 3 -> 0; matrix products, arithmetic and copies ran while one was open for 2% -> 0% of each run, Pallas kernels for 0% -> 0%
where the time goes in v2:
time: 162 us; the launch traced here: 161 us
  Pallas kernels  156 us (96%)
  local copies, waits for them, and re-layouts  2.93 us (2%)
  between operations  1.93 us (1%)
    pallas_call x1, Pallas kernels, local(): pl.pallas_call(kernel, out_shape=(out, out), in_specs=[anyspec] * 4 + [sm...  156 us

profile of v2, /device:TPU:1, one launch (start us, length us, event | category | flops | bytes accessed | tf_op | source)
XLA Modules:
  0.0 161.3 jit_solution(17901211063266192558)
XLA Ops:
  1.9 156.5 %shard_map.86 = (f32[4144,128]{1,0:T(8,128)S(1)}, f32[4144,128]{1,0:T(8,128)S(1)}) custom-call(bf16[1024,3584]{1,0:T(8,128)(2,1)} %acts.1, bf16[2368,1024]{1,0:T(8,128)(2,1)} %bitcast.5, f32[224,2368]{1,0:T(8,128)} %hess.1, f32[224,2368]{1,0:T(8,128)} %mom.1, f32[28]{0:T(128)} %gamma_table.1, s32[1]{0:T(128)S(6)} %copy.13.layer, s32[1]{0:T(128)S(6)} %copy.14.steps), custom_call_target="tpu_custom_call" | custom-call | tf_op jit(solution)/shard_map/pallas_call | solution.py:505
  158.4 1.5 copy.11
  159.9 1.5 copy.12

commit v3 on v2

--- a/solution.py
+++ b/solution.py
@@ -16,7 +16,7 @@
 HALF = NX - 1
 NS = 4
 ND = 3
-NQ = 4
+NQ = 6
 NH = 6
 
 
@@ -438,7 +438,7 @@
             for c in az_copies(i):
                 c.start()
 
-        u4 = t - 5
+        u4 = t - 6
 
         @within(u4, 0, NX)
         def _():
@@ -456,7 +456,7 @@
             for c in a_copies(u4):
                 c.start()
 
-        u5 = t - 7
+        u5 = t - 9
 
         @pl.when(u5 >= 0)
         def _():
@@ -476,7 +476,7 @@
                         (hm_buf[j, HALF, 0], hm_buf[j + 1, HALF, 0]), (hm_buf[j, HALF, 1], hm_buf[j + 1, HALF, 1]))))
         return carry
 
-    lax.fori_loop(1, NT + 7, body, 0)
+    lax.fori_loop(1, NT + 9, body, 0)
 
     for n in range(NX - NS, NX):
         for c in half_copies() if n == HALF else x_copies(n):

time: 162 us -> 160 us (0.988)
  no operation moved by 1% of the time
where the time goes in v3:
time: 160 us
  Pallas kernels  155 us (97%)
  local copies, waits for them, and re-layouts  2.93 us (2%)
  between operations  1.93 us (1%)
    pallas_call x1, Pallas kernels, local(): pl.pallas_call(kernel, out_shape=(out, out), in_specs=[anyspec] * 4 + [sm...  155 us

profile of v3, /device:TPU:1, one launch (start us, length us, event | category | flops | bytes accessed | tf_op | source)
XLA Modules:
  0.0 159.8 jit_solution(11618487754562639473)
XLA Ops:
  1.9 155.0 %shard_map.86 = (f32[4144,128]{1,0:T(8,128)S(1)}, f32[4144,128]{1,0:T(8,128)S(1)}) custom-call(bf16[1024,3584]{1,0:T(8,128)(2,1)} %acts.1, bf16[2368,1024]{1,0:T(8,128)(2,1)} %bitcast.5, f32[224,2368]{1,0:T(8,128)} %hess.1, f32[224,2368]{1,0:T(8,128)} %mom.1, f32[28]{0:T(128)} %gamma_table.1, s32[1]{0:T(128)S(6)} %copy.13.layer, s32[1]{0:T(128)S(6)} %copy.14.steps), custom_call_target="tpu_custom_call" | custom-call | tf_op jit(solution)/shard_map/pallas_call | solution.py:505
  156.9 1.5 copy.11
  158.4 1.5 copy.12

commit v4 on v3

--- a/solution.py
+++ b/solution.py
@@ -146,20 +146,21 @@
     def a_copies(n):
         s = lax.rem(n, NQ)
         out = []
-        for k in range(1, 4):
+        for k in (2, 1, 3):
             to = lax.rem(y + k, 4)
             out.append(remote(a_send.at[s, 0, window(to), :], g_buf.at[tn, n], a_ssem.at[s, k - 1], a_rsem.at[n], (dp, to * 2 + h)))
-        for k in range(4):
+        for k in (2, 1, 3, 0):
             to = lax.rem(y + k, 4)
             out.append(remote(a_send.at[s, 1, window(to), :], g_buf.at[tn, n], a_ssem.at[s, 3 + k], a_rsem.at[n], (flip_dp, to * 2 + 1 - h)))
         return out
 
     def az_copies(i):
         out = []
-        for k in range(1, 8):
-            to = lax.rem(tn + k, 8)
-            out.append(remote(az.at[i, lax.rem(to, 2), window(lax.div(to, 2)), :], g_buf.at[tn, NX + i],
-                              az_ssem.at[i, k - 1], a_rsem.at[NX + i], (dp, to)))
+        far_first = ((2, 1), (1, 1), (3, 1), (2, 0), (0, 1), (1, 0), (3, 0))
+        for slot, (dy, dh) in enumerate(far_first):
+            to_y, to_h = lax.rem(y + dy, 4), lax.rem(h + dh, 2)
+            out.append(remote(az.at[i, to_h, window(to_y), :], g_buf.at[tn, NX + i],
+                              az_ssem.at[i, slot], a_rsem.at[NX + i], (dp, to_y * 2 + to_h)))
         return out
 
     def h_copies(n):

time: 160 us -> 160 us (level)
  no operation moved by 1% of the time
where the time goes in v4:
time: 160 us
  Pallas kernels  155 us (97%)
  local copies, waits for them, and re-layouts  2.93 us (2%)
  between operations  1.93 us (1%)
    pallas_call x1, Pallas kernels, local(): pl.pallas_call(kernel, out_shape=(out, out), in_specs=[anyspec] * 4 + [sm...  155 us

profile of v4, /device:TPU:1, one launch (start us, length us, event | category | flops | bytes accessed | tf_op | source)
XLA Modules:
  0.0 159.6 jit_solution(13891265652652040837)
XLA Ops:
  1.9 154.7 %shard_map.86 = (f32[4144,128]{1,0:T(8,128)S(1)}, f32[4144,128]{1,0:T(8,128)S(1)}) custom-call(bf16[1024,3584]{1,0:T(8,128)(2,1)} %acts.1, bf16[2368,1024]{1,0:T(8,128)(2,1)} %bitcast.5, f32[224,2368]{1,0:T(8,128)} %hess.1, f32[224,2368]{1,0:T(8,128)} %mom.1, f32[28]{0:T(128)} %gamma_table.1, s32[1]{0:T(128)S(6)} %copy.13.layer, s32[1]{0:T(128)S(6)} %copy.14.steps), custom_call_target="tpu_custom_call" | custom-call | tf_op jit(solution)/shard_map/pallas_call | solution.py:506
  156.7 1.5 copy.11
  158.1 1.5 copy.12
